TPU v7x, 32 devices: a whole 2x2x4 slice. The times are simulated.
32 devices in a mesh: row: 4 (over y, x), col: 8 (over z, core).
Axes of the slice: x: 2, y: 2, z: 4, core: 2. Of those that a mesh axis runs over, the one named last changes fastest.
Arguments:
- trial: bfloat16 [2, 512, 2048], P(None, 'row', 'col'), may hold values from -6 to 6
- val_energy: float32 [512], P('row'), may hold values from -1 to 0
- cond_energy: float32 [2048], P('col'), may hold values from 0.5 to 2
- val_orbitals: bfloat16 [512, 20480], P('col', 'row'), may hold values from -0.25 to 0.25
- cond_orbitals: bfloat16 [2048, 20480], P('row', 'col'), may hold values from -0.125 to 0.125
- screening: bfloat16 [20480, 20480], P('row', 'col'), may hold values from -0.29882812 to 0.29882812
Outputs:
- applied: float32 [2, 512, 2048], P(None, 'row', 'col')
All inputs are finite; a program needn't handle non-finite values.
Results may differ from a plain program's by a relative error of at most 0.0028.
Values may be sent and summed in bfloat16 or wider, within the bound.
No kernel may reach another device: no remote copies, remote signals or barrier semaphores. Data moves between devices by JAX's collectives and lax.ppermute only.
A program may use at most 128 MiB of HBM per device.

v0:
```python
import jax
import jax.numpy as jnp
from jax import lax
from jax.sharding import PartitionSpec as P


def local(trial, val_energy, cond_energy, val_orbitals, cond_orbitals, screening):
    full_trial = lax.all_gather(trial, "col", axis=2, tiled=True)
    cond_full = lax.all_gather(cond_orbitals, "row", axis=0, tiled=True)
    val_full = lax.all_gather(val_orbitals, "col", axis=0, tiled=True)
    encoded = jnp.einsum(
        "bvc,cn->bvn", full_trial, cond_full, preferred_element_type=jnp.float32
    ).astype(jnp.bfloat16)
    scr_float = screening.astype(jnp.float32)

    def decode_part(enc_part):
        val_rows = val_full
        moments = jnp.einsum(
            "vm,bvn->bmn",
            val_rows,
            lax.all_gather(enc_part, "row", axis=1, tiled=True),
            preferred_element_type=jnp.float32,
        )
        screened = (scr_float[None] * moments).astype(jnp.bfloat16)
        val_rows = val_full
        half = lax.psum_scatter(
            jnp.einsum("vm,bmn->vbn", val_rows, screened, preferred_element_type=jnp.float32),
            "row",
            scatter_dimension=0,
            tiled=True,
        ).astype(jnp.bfloat16)
        partial_kernel = jnp.einsum(
            "vbn,cn->bvc", half, cond_full, preferred_element_type=jnp.float32
        )
        return lax.psum_scatter(partial_kernel, "col", scatter_dimension=2, tiled=True)

    pieces = [decode_part(encoded[b : b + 1]) for b in range(trial.shape[0])]
    kernel = jnp.concatenate(pieces, axis=0)
    gaps = cond_energy[None, None, :] - val_energy[None, :, None]
    return gaps * trial.astype(jnp.float32) + kernel


def solution(mesh):
    placed = (
        P(None, "row", "col"),
        P("row"),
        P("col"),
        P("col", "row"),
        P("row", "col"),
        P("row", "col"),
    )
    return jax.shard_map(
        local, mesh=mesh, in_specs=placed, out_specs=P(None, "row", "col"), check_vma=False
    )
```

profile of v0, /device:TPU:0, one launch (start us, length us, event | category | flops | bytes accessed | tf_op | source)
XLA Modules:
  0.0 484.8 jit_solution(12320645691943452132)
XLA Ops:
  6.5 0.7 all-gather.6.cloned.1.call-update
  7.3 0.0 all-gather.8.cloned.1.call-start
  7.3 0.7 all-gather.8.cloned.1.call-update
  8.0 0.0 all-gather.12.cloned.1.call-start
  8.1 0.7 all-gather.12.cloned.1.call-update
  8.7 0.0 all-gather.10.cloned.1.call-start
  8.8 26.8 %all-gather.6.cloned.1.call-done = bf16[2,128,2048]{2,1,0:T(8,128)(2,1)} async-done(((bf16[2,128,256]{2,1,0:T(8,128)(2,1)}), bf16[2,128,2048]{2,1,0:T(8,128)(2,1)}) %all-gather.6.cloned.1.call-update) | async-done | bytes 1048592 | tf_op jit(solution)/shard_map/all_gather | solution.py:8
  35.6 105.6 %all-gather.8.cloned.1.call-done = bf16[2048,2560]{1,0:T(8,128)(2,1)} async-done(((bf16[512,2560]{1,0:T(8,128)(2,1)}), bf16[2048,2560]{1,0:T(8,128)(2,1)}) %all-gather.8.cloned.1.call-update) | async-done | bytes 10485776 | tf_op jit(solution)/shard_map/all_gather | solution.py:9
  141.1 7.2 %fusion.14 = bf16[2,128,2560]{2,1,0:T(8,128)(2,1)S(1)} fusion(bf16[2,128,2048]{2,1,0:T(8,128)(2,1)} %all-gather.6.cloned.1.call-done, bf16[2048,2560]{1,0:T(8,128)(2,1)} %all-gather.8.cloned.1.call-done), kind=kOutput, calls=%fused_computation.12 | convolution fusion | flops 2685009920 | bytes 12845056 | tf_op jit(solution)/shard_map/bvc,cn->bvn/dot_general | solution.py:11
  148.3 1.1 fusion.25
  149.4 0.0 all-gather.10.cloned.1.call-update
  149.5 0.0 all-gather.14.cloned.1.call-start
  149.5 34.4 %copy.7 = bf16[5120,2560]{0,1:T(8,128)(2,1)} copy(bf16[5120,2560]{1,0:T(8,128)(2,1)} %param.11) | data formatting | bytes 52428800 | tf_op args[5]
  183.9 0.0 all-gather.14.cloned.1.call-update
  183.9 0.0 reduce-scatter.5.cloned.1.call-start
  184.0 14.8 %all-gather.12.cloned.1.call-done = bf16[512,5120]{1,0:T(8,128)(2,1)} async-done(((bf16[64,5120]{1,0:T(8,128)(2,1)}), bf16[512,5120]{1,0:T(8,128)(2,1)}) %all-gather.12.cloned.1.call-update) | async-done | bytes 5242896 | tf_op jit(solution)/shard_map/all_gather | solution.py:10
  198.8 40.0 %all-gather.10.cloned.1.call-done = bf16[1,512,2560]{2,1,0:T(8,128)(2,1)} async-done(((bf16[1,128,2560]{2,1,0:T(8,128)(2,1)}), bf16[1,512,2560]{2,1,0:T(8,128)(2,1)}) %all-gather.10.cloned.1.call-update) | async-done | bytes 2621456 | tf_op jit(solution)/shard_map/all_gather | solution.py:21
  238.8 37.3 %fusion.8 = f32[512,1,2560]{0,2,1:T(8,128)} fusion(bf16[512,5120]{1,0:T(8,128)(2,1)} %all-gather.12.cloned.1.call-done, bf16[5120,2560]{0,1:T(8,128)(2,1)} %copy.7, bf16[1,512,2560]{2,1,0:T(8,128)(2,1)} %all-gather.10.cloned.1.call-done), kind=kOutput, calls=%fused_computation.10 | convolution fusion | flops 26882867200 | bytes 39321600 | tf_op jit(solution)/shard_map/vm,bmn->vbn/dot_general | solution.py:27
  276.1 0.2 reduce-scatter.9.cloned.1.call-start
  276.3 3.7 all-gather.14.cloned.1.call-done
  280.0 37.3 %fusion.11 = f32[512,1,2560]{0,2,1:T(8,128)} fusion(bf16[512,5120]{1,0:T(8,128)(2,1)} %all-gather.12.cloned.1.call-done, bf16[5120,2560]{0,1:T(8,128)(2,1)} %copy.7, bf16[1,512,2560]{2,1,0:T(8,128)(2,1)} %all-gather.14.cloned.1.call-done), kind=kOutput, calls=%fused_computation.11 | convolution fusion | flops 26882867200 | bytes 39321600 | tf_op jit(solution)/shard_map/vm,bmn->vbn/dot_general | solution.py:27
  317.3 0.0 reduce-scatter.7.cloned.1.call-start
  317.3 26.9 %reduce-scatter.5.cloned.1.call-done = f32[128,1,2560]{0,2,1:T(8,128)} async-done(((f32[512,1,2560]{0,2,1:T(8,128)}), f32[128,1,2560]{0,2,1:T(8,128)}) %reduce-scatter.5.cloned.1.call-update) | async-done | bytes 1310736 | tf_op jit(solution)/shard_map/reduce_scatter | solution.py:26
  344.2 8.9 %convolution_bitcast_fusion.1 = f32[1,128,2048]{2,1,0:T(8,128)} fusion(bf16[2048,2560]{1,0:T(8,128)(2,1)} %all-gather.8.cloned.1.call-done, f32[128,1,2560]{0,2,1:T(8,128)} %reduce-scatter.5.cloned.1.call-done), kind=kOutput, calls=%fused_computation.16 | convolution fusion | flops 1342504960 | bytes 12845056 | tf_op jit(solution)/shard_map/vbn,cn->bvc/dot_general | solution.py:32
  353.1 0.0 reduce-scatter.7.cloned.1.call-update
  353.2 0.0 reduce-scatter.11.cloned.1.call-start
  353.2 55.3 %reduce-scatter.9.cloned.1.call-done = f32[128,1,2560]{0,2,1:T(8,128)} async-done(((f32[512,1,2560]{0,2,1:T(8,128)}), f32[128,1,2560]{0,2,1:T(8,128)}) %reduce-scatter.9.cloned.1.call-update) | async-done | bytes 1310736 | tf_op jit(solution)/shard_map/reduce_scatter | solution.py:26
  408.6 9.0 %convolution_bitcast_fusion = f32[1,128,2048]{2,1,0:T(8,128)} fusion(bf16[2048,2560]{1,0:T(8,128)(2,1)} %all-gather.8.cloned.1.call-done, f32[128,1,2560]{0,2,1:T(8,128)} %reduce-scatter.9.cloned.1.call-done), kind=kOutput, calls=%fused_computation.15 | convolution fusion | flops 1342504960 | bytes 12845056 | tf_op jit(solution)/shard_map/vbn,cn->bvc/dot_general | solution.py:32
  417.5 0.1 broadcast_subtract_fusion
  417.6 25.8 %reduce-scatter.7.cloned.1.call-done = f32[1,128,256]{2,1,0:T(8,128)} async-done(((f32[1,128,2048]{2,1,0:T(8,128)}), f32[1,128,256]{2,1,0:T(8,128)}) %reduce-scatter.7.cloned.1.call-update) | async-done | bytes 131088 | tf_op jit(solution)/shard_map/reduce_scatter | solution.py:35
  443.5 33.1 %reduce-scatter.11.cloned.1.call-done = f32[1,128,256]{2,1,0:T(8,128)} async-done(((f32[1,128,2048]{2,1,0:T(8,128)}), f32[1,128,256]{2,1,0:T(8,128)}) %reduce-scatter.11.cloned.1.call-update) | async-done | bytes 131088 | tf_op jit(solution)/shard_map/reduce_scatter | solution.py:35
  476.5 1.7 maximum_add_fusion
  (10 shorter events, 0.1 us)
Async XLA Ops:
  6.5 29.0 %all-gather.6.cloned.1.call-start = ((), (), s32[]{:S(2)}) async-start(), calls=%async_computation.4 | async-start | bytes 1179648 | tf_op jit(solution)/shard_map/all_gather | solution.py:8
  7.3 133.9 %all-gather.8.cloned.1.call-start = ((), (), s32[]{:S(2)}) async-start(), calls=%async_computation.5 | async-start | bytes 13107200 | tf_op jit(solution)/shard_map/all_gather | solution.py:9
  8.0 190.8 %all-gather.12.cloned.1.call-start = ((), (), s32[]{:S(2)}) async-start(), calls=%async_computation.7 | async-start | bytes 5898240 | tf_op jit(solution)/shard_map/all_gather | solution.py:10
  8.7 230.0 %all-gather.10.cloned.1.call-start = ((), (), s32[]{:S(2)}) async-start(), calls=%async_computation.6 | async-start | bytes 3276800 | tf_op jit(solution)/shard_map/all_gather | solution.py:21
  149.5 130.5 %all-gather.14.cloned.1.call-start = ((), (), s32[]{:S(2)}) async-start(), calls=%async_computation.10 | async-start | bytes 3276800 | tf_op jit(solution)/shard_map/all_gather | solution.py:21
  183.9 160.3 %reduce-scatter.5.cloned.1.call-start = ((), (), s32[]{:S(2)}) async-start(), calls=%async_computation.8 | async-start | bytes 6553600 | tf_op jit(solution)/shard_map/reduce_scatter | solution.py:26
  276.1 132.5 %reduce-scatter.9.cloned.1.call-start = ((), (), s32[]{:S(2)}) async-start(), calls=%async_computation.11 | async-start | bytes 6553600 | tf_op jit(solution)/shard_map/reduce_scatter | solution.py:26
  317.3 126.2 %reduce-scatter.7.cloned.1.call-start = ((), (), s32[]{:S(2)}) async-start(), calls=%async_computation.9 | async-start | bytes 1179648 | tf_op jit(solution)/shard_map/reduce_scatter | solution.py:35
  353.1 64.4 %copy-start.1 = (f32[256]{0:T(256)S(1)}, f32[256]{0:T(256)}, u32[]{:S(2)}) copy-start(f32[256]{0:T(256)} %param.8) | copy-start | bytes 3076
  353.1 64.4 %copy-start.2 = (f32[128]{0:T(128)S(1)}, f32[128]{0:T(128)}, u32[]{:S(2)}) copy-start(f32[128]{0:T(128)} %param.7) | copy-start | bytes 1540
  353.1 123.4 %copy-start = (bf16[2,128,256]{2,1,0:T(8,128)(2,1)S(1)}, bf16[2,128,256]{2,1,0:T(8,128)(2,1)}, u32[]{:S(2)}) copy-start(bf16[2,128,256]{2,1,0:T(8,128)(2,1)} %param.6) | copy-start | bytes 393220
  353.2 123.4 %reduce-scatter.11.cloned.1.call-start = ((), (), s32[]{:S(2)}) async-start(), calls=%async_computation.12 | async-start | bytes 1179648 | tf_op jit(solution)/shard_map/reduce_scatter | solution.py:35
Sparse Core Ops, SparseCore 0:
  8.9 26.5 all-gather.5
  37.4 103.6 all-gather.7
  142.8 55.9 all-gather.11
  200.5 38.2 all-gather.9
  240.5 39.4 all-gather.13
  282.8 61.3 reduce-scatter.4
  347.2 61.3 reduce-scatter.8
  410.8 32.5 reduce-scatter.6
  445.7 30.7 reduce-scatter.10
where the time goes:
time: 486 us; the launch traced here: 485 us
  waiting for transfers between devices  334 us (69%)
  matrix products  99.5 us (20%)
  local copies, waits for them, and re-layouts  35.6 us (7%)
  between operations  13.3 us (3%)
    all_gather x1, waiting for transfers between devices, local(): cond_full = lax.all_gather(cond_orbitals, 'row', axis=0, tiled=True)  106 us
    reduce_scatter x2, waiting for transfers between devices, decode_part(): lax.psum_scatter(jnp.einsum('vm,bmn->vbn', val_rows, screened, preferred_...  82.2 us
    dot_general x2, matrix products, decode_part(): jnp.einsum('vm,bmn->vbn', val_rows, screened, preferred_element_type=jnp....  74.5 us
    reduce_scatter x2, waiting for transfers between devices, decode_part(): lax.psum_scatter(partial_kernel, 'col', scatter_dimension=2, tiled=True)  58.9 us
    all_gather x2, waiting for transfers between devices, decode_part(): lax.all_gather(enc_part, 'row', axis=1, tiled=True)  43.7 us
    unnamed x7, local copies, waits for them, and re-layouts  34.4 us
    all_gather x1, waiting for transfers between devices, local(): full_trial = lax.all_gather(trial, 'col', axis=2, tiled=True)  26.8 us
    dot_general x2, matrix products, decode_part(): jnp.einsum('vbn,cn->bvc', half, cond_full, preferred_element_type=jnp.flo...  17.8 us
  transfers between devices with their start and end apart: 9, of which 9 were waited for; matrix products, arithmetic and copies ran while one was open for 28% of the time, Pallas kernels for 0%

commit v1 on v0

--- a/solution.py
+++ b/solution.py
@@ -4,12 +4,35 @@
 from jax.sharding import PartitionSpec as P
 
 
+def summed_both_ways(x, axis, dim, contribution):
+    size, index, rows = (lax.axis_size(axis), lax.axis_index(axis), x.shape[dim])
+    right = [(i, (i + 1) % size) for i in range(size)]
+    left = [(i, (i - 1) % size) for i in range(size)]
+    middle = size // 2
+    from_left = from_right = x
+    total = contribution(x, index * rows)
+    for step in range(1, middle + 1):
+        from_left = lax.ppermute(from_left, axis, right)
+        if step < size - middle:
+            from_right = lax.ppermute(from_right, axis, left)
+            total = total + contribution(from_right, (index + step) % size * rows)
+        total = total + contribution(from_left, (index - step) % size * rows)
+    return total
+
+
 def local(trial, val_energy, cond_energy, val_orbitals, cond_orbitals, screening):
-    full_trial = lax.all_gather(trial, "col", axis=2, tiled=True)
     cond_full = lax.all_gather(cond_orbitals, "row", axis=0, tiled=True)
     val_full = lax.all_gather(val_orbitals, "col", axis=0, tiled=True)
-    encoded = jnp.einsum(
-        "bvc,cn->bvn", full_trial, cond_full, preferred_element_type=jnp.float32
+    encoded = summed_both_ways(
+        trial,
+        "col",
+        2,
+        lambda own_block, at: jnp.einsum(
+            "bvc,cn->bvn",
+            own_block,
+            lax.dynamic_slice_in_dim(cond_full, at, own_block.shape[2], axis=0),
+            preferred_element_type=jnp.float32,
+        ),
     ).astype(jnp.bfloat16)
     scr_float = screening.astype(jnp.float32)
 

time: 486 us -> 463 us (0.953)
  waiting for transfers between devices: 334 us -> 299 us
  starting transfers between devices: 0.51 us -> 12.3 us
    all_gather x1 -> x0, waiting for transfers between devices: 26.8 us -> none  [local(): full_trial = lax.all_gather(trial, 'col', axis=2, tiled=True)]
    all_gather x1, waiting for transfers between devices: 106 us -> 86.2 us  [local(): cond_full = lax.all_gather(cond_orbitals, 'row', axis=0, tiled=True)]
    ppermute x0 -> x7, starting transfers between devices: none -> 11.8 us  [the longest x3 11.3 us: summed_both_ways(): from_right = lax.ppermute(from_right, axis, left)]
    ppermute x0 -> x7, waiting for transfers between devices: none -> 8.83 us  [the longest x4 8.73 us: summed_both_ways(): from_left = lax.ppermute(from_left, axis, right)]
    unnamed x7 -> x10, local copies, waits for them, and re-layouts: 34.4 us -> 37.2 us
  transfers between devices with their start and end apart: 9 -> 15, of which waited for: 9 -> 12; matrix products, arithmetic and copies ran while one was open for 28% -> 28% of each run, Pallas kernels for 0% -> 0%
where the time goes in v1:
time: 463 us; the launch traced here: 462 us
  waiting for transfers between devices  299 us (65%)
  matrix products  97 us (21%)
  local copies, waits for them, and re-layouts  38.3 us (8%)
  between operations  13.6 us (3%)
  starting transfers between devices  12.3 us (3%)
    all_gather x1, waiting for transfers between devices, local(): cond_full = lax.all_gather(cond_orbitals, 'row', axis=0, tiled=True)  86.2 us
    reduce_scatter x2, waiting for transfers between devices, decode_part(): lax.psum_scatter(jnp.einsum('vm,bmn->vbn', val_rows, screened, preferred_...  84.3 us
    dot_general x2, matrix products, decode_part(): jnp.einsum('vm,bmn->vbn', val_rows, screened, preferred_element_type=jnp....  74 us
    reduce_scatter x2, waiting for transfers between devices, decode_part(): lax.psum_scatter(partial_kernel, 'col', scatter_dimension=2, tiled=True)  60.9 us
    all_gather x2, waiting for transfers between devices, decode_part(): lax.all_gather(enc_part, 'row', axis=1, tiled=True)  43.8 us
    unnamed x10, local copies, waits for them, and re-layouts  37.2 us
    all_gather x1, waiting for transfers between devices, local(): val_full = lax.all_gather(val_orbitals, 'col', axis=0, tiled=True)  14.5 us
    dot_general x2, matrix products, decode_part(): jnp.einsum('vbn,cn->bvc', half, cond_full, preferred_element_type=jnp.flo...  13.9 us
  transfers between devices with their start and end apart: 15, of which 12 were waited for; matrix products, arithmetic and copies ran while one was open for 28% of the time, Pallas kernels for 0%

profile of v1, /device:TPU:0, one launch (start us, length us, event | category | flops | bytes accessed | tf_op | source)
XLA Modules:
  0.0 462.4 jit_solution(18012152841609825693)
XLA Ops:
  6.5 4.4 copy.8
  11.0 0.7 all-gather.9.cloned.1.call-update
  11.9 0.5 collective-permute-start.1
  12.3 4.1 collective-permute-start
  16.4 2.7 collective-permute-done.1
  19.1 3.5 collective-permute-start.2
  22.7 3.3 collective-permute-done.3
  26.1 3.7 collective-permute-start.4
  29.8 2.7 collective-permute-done.5
  32.5 86.2 %all-gather.5.cloned.1.call-done = bf16[2048,2560]{0,1:T(8,128)(2,1)} async-done(((bf16[512,2560]{0,1:T(8,128)(2,1)}), bf16[2048,2560]{0,1:T(8,128)(2,1)}) %all-gather.5.cloned.1.call-update) | async-done | bytes 10485776 | tf_op jit(solution)/shard_map/all_gather | solution.py:24
  118.7 1.8 fusion.29
  120.5 2.0 fusion.24
  122.5 2.4 convolution_add_fusion.4
  125.3 0.6 convolution_add_fusion.3
  125.9 0.6 fusion.12
  126.5 0.5 fusion.21
  127.1 0.6 fusion.13
  127.7 0.5 fusion.15
  128.2 1.2 fusion.51
  129.5 32.3 %copy.7 = bf16[5120,2560]{0,1:T(8,128)(2,1)} copy(bf16[5120,2560]{1,0:T(8,128)(2,1)} %param.11) | data formatting | bytes 52428800 | tf_op args[5]
  161.8 14.5 %all-gather.9.cloned.1.call-done = bf16[512,5120]{1,0:T(8,128)(2,1)} async-done(((bf16[64,5120]{1,0:T(8,128)(2,1)}), bf16[512,5120]{1,0:T(8,128)(2,1)}) %all-gather.9.cloned.1.call-update) | async-done | bytes 5242896 | tf_op jit(solution)/shard_map/all_gather | solution.py:25
  176.3 40.0 %all-gather.7.cloned.1.call-done = bf16[1,512,2560]{1,2,0:T(8,128)(2,1)} async-done(((bf16[1,128,2560]{1,2,0:T(8,128)(2,1)}), bf16[1,512,2560]{1,2,0:T(8,128)(2,1)}) %all-gather.7.cloned.1.call-update) | async-done | bytes 2621456 | tf_op jit(solution)/shard_map/all_gather | solution.py:44
  216.3 37.0 %fusion.6 = f32[512,1,2560]{0,2,1:T(8,128)} fusion(bf16[512,5120]{1,0:T(8,128)(2,1)} %all-gather.9.cloned.1.call-done, bf16[5120,2560]{0,1:T(8,128)(2,1)} %copy.7, bf16[1,512,2560]{1,2,0:T(8,128)(2,1)} %all-gather.7.cloned.1.call-done), kind=kOutput, calls=%fused_computation.8 | convolution fusion | flops 26882867200 | bytes 39321600 | tf_op jit(solution)/shard_map/vm,bmn->vbn/dot_general | solution.py:50
  253.6 3.8 all-gather.11.cloned.1.call-done
  257.4 37.0 %fusion.9 = f32[512,1,2560]{0,2,1:T(8,128)} fusion(bf16[512,5120]{1,0:T(8,128)(2,1)} %all-gather.9.cloned.1.call-done, bf16[5120,2560]{0,1:T(8,128)(2,1)} %copy.7, bf16[1,512,2560]{1,2,0:T(8,128)(2,1)} %all-gather.11.cloned.1.call-done), kind=kOutput, calls=%fused_computation.9 | convolution fusion | flops 26882867200 | bytes 39321600 | tf_op jit(solution)/shard_map/vm,bmn->vbn/dot_general | solution.py:50
  294.5 27.1 %reduce-scatter.5.cloned.1.call-done = f32[128,1,2560]{0,2,1:T(8,128)} async-done(((f32[512,1,2560]{0,2,1:T(8,128)}), f32[128,1,2560]{0,2,1:T(8,128)}) %reduce-scatter.5.cloned.1.call-update) | async-done | bytes 1310736 | tf_op jit(solution)/shard_map/reduce_scatter | solution.py:49
  321.6 6.9 %convolution_bitcast_fusion.1 = f32[1,128,2048]{2,1,0:T(8,128)} fusion(bf16[2048,2560]{0,1:T(8,128)(2,1)} %all-gather.5.cloned.1.call-done, f32[128,1,2560]{0,2,1:T(8,128)} %reduce-scatter.5.cloned.1.call-done), kind=kOutput, calls=%fused_computation.22 | convolution fusion | flops 1342504960 | bytes 12845056 | tf_op jit(solution)/shard_map/vbn,cn->bvc/dot_general | solution.py:55
  328.6 57.2 %reduce-scatter.9.cloned.1.call-done = f32[128,1,2560]{0,2,1:T(8,128)} async-done(((f32[512,1,2560]{0,2,1:T(8,128)}), f32[128,1,2560]{0,2,1:T(8,128)}) %reduce-scatter.9.cloned.1.call-update) | async-done | bytes 1310736 | tf_op jit(solution)/shard_map/reduce_scatter | solution.py:49
  385.8 7.0 %convolution_bitcast_fusion = f32[1,128,2048]{2,1,0:T(8,128)} fusion(bf16[2048,2560]{0,1:T(8,128)(2,1)} %all-gather.5.cloned.1.call-done, f32[128,1,2560]{0,2,1:T(8,128)} %reduce-scatter.9.cloned.1.call-done), kind=kOutput, calls=%fused_computation.21 | convolution fusion | flops 1342504960 | bytes 12845056 | tf_op jit(solution)/shard_map/vbn,cn->bvc/dot_general | solution.py:55
  392.9 27.8 %reduce-scatter.7.cloned.1.call-done = f32[1,128,256]{2,1,0:T(8,128)} async-done(((f32[1,128,2048]{2,1,0:T(8,128)}), f32[1,128,256]{2,1,0:T(8,128)}) %reduce-scatter.7.cloned.1.call-update) | async-done | bytes 131088 | tf_op jit(solution)/shard_map/reduce_scatter | solution.py:58
  420.7 33.1 %reduce-scatter.11.cloned.1.call-done = f32[1,128,256]{2,1,0:T(8,128)} async-done(((f32[1,128,2048]{2,1,0:T(8,128)}), f32[1,128,256]{2,1,0:T(8,128)}) %reduce-scatter.11.cloned.1.call-update) | async-done | bytes 131088 | tf_op jit(solution)/shard_map/reduce_scatter | solution.py:58
  453.8 1.7 maximum_add_fusion
  (31 shorter events, 1.2 us)
Async XLA Ops:
  6.5 112.1 %all-gather.5.cloned.1.call-start = ((), (), s32[]{:S(2)}) async-start(), calls=%async_computation.4 | async-start | bytes 13107200 | tf_op jit(solution)/shard_map/all_gather | solution.py:24
  10.9 0.9 copy-start.1
  11.0 165.3 %all-gather.9.cloned.1.call-start = ((), (), s32[]{:S(2)}) async-start(), calls=%async_computation.6 | async-start | bytes 5898240 | tf_op jit(solution)/shard_map/all_gather | solution.py:25
  11.7 204.6 %all-gather.7.cloned.1.call-start = ((), (), s32[]{:S(2)}) async-start(), calls=%async_computation.5 | async-start | bytes 3276800 | tf_op jit(solution)/shard_map/all_gather | solution.py:44
  11.9 7.3 %collective-permute-start.1 = (bf16[2,128,256]{2,1,0:T(8,128)(2,1)S(1)}, bf16[2,128,256]{2,1,0:T(8,128)(2,1)S(1)}, u32[]{:S(2)}, u32[]{:S(2)}) collective-permute-start(bf16[2,128,256]{2,1,0:T(8,128)(2,1)S(1)} %copy-done.1), channel_id=1, source_target_pairs={{0,1},{1,2},{2,3},{3,4},{4,5},{5,6},{6,7},{7,0},{8,9},{9,10},{10,1... | collective-permute-start | bytes 393224 | tf_op jit(solution)/shard_map/ppermute | solution.py:15
  12.3 6.8 %collective-permute-start = (bf16[2,128,256]{2,1,0:T(8,128)(2,1)S(1)}, bf16[2,128,256]{2,1,0:T(8,128)(2,1)S(1)}, u32[]{:S(2)}, u32[]{:S(2)}) collective-permute-start(bf16[2,128,256]{2,1,0:T(8,128)(2,1)S(1)} %copy-done.1), channel_id=1, source_target_pairs={{0,7},{1,0},{2,1},{3,2},{4,3},{5,4},{6,5},{7,6},{8,15},{9,8},{10,9... | collective-permute-start | bytes 393224 | tf_op jit(solution)/shard_map/ppermute | solution.py:17
  19.1 6.9 %collective-permute-start.3 = (bf16[2,128,256]{2,1,0:T(8,128)(2,1)S(1)}, bf16[2,128,256]{2,1,0:T(8,128)(2,1)S(1)}, u32[]{:S(2)}, u32[]{:S(2)}) collective-permute-start(bf16[2,128,256]{2,1,0:T(8,128)(2,1)S(1)} %collective-permute-done.1), channel_id=1, source_target_pairs={{0,1},{1,2},{2,3},{3,4},{4,5},{5,6},{6,7},{7,0},{8,9},{9,10},{10,1... | collective-permute-start | bytes 393224 | tf_op jit(solution)/shard_map/ppermute | solution.py:15
  19.1 7.0 %collective-permute-start.2 = (bf16[2,128,256]{2,1,0:T(8,128)(2,1)S(1)}, bf16[2,128,256]{2,1,0:T(8,128)(2,1)S(1)}, u32[]{:S(2)}, u32[]{:S(2)}) collective-permute-start(bf16[2,128,256]{2,1,0:T(8,128)(2,1)S(1)} %collective-permute-done), channel_id=1, source_target_pairs={{0,7},{1,0},{2,1},{3,2},{4,3},{5,4},{6,5},{7,6},{8,15},{9,8},{10,9... | collective-permute-start | bytes 393224 | tf_op jit(solution)/shard_map/ppermute | solution.py:17
  26.0 6.5 %collective-permute-start.5 = (bf16[2,128,256]{2,1,0:T(8,128)(2,1)S(1)}, bf16[2,128,256]{2,1,0:T(8,128)(2,1)S(1)}, u32[]{:S(2)}, u32[]{:S(2)}) collective-permute-start(bf16[2,128,256]{2,1,0:T(8,128)(2,1)S(1)} %collective-permute-done.3), channel_id=1, source_target_pairs={{0,1},{1,2},{2,3},{3,4},{4,5},{5,6},{6,7},{7,0},{8,9},{9,10},{10,1... | collective-permute-start | bytes 393224 | tf_op jit(solution)/shard_map/ppermute | solution.py:15
  26.1 101.0 %collective-permute-start.4 = (bf16[2,128,256]{2,1,0:T(8,128)(2,1)S(1)}, bf16[2,128,256]{2,1,0:T(8,128)(2,1)S(1)}, u32[]{:S(2)}, u32[]{:S(2)}) collective-permute-start(bf16[2,128,256]{2,1,0:T(8,128)(2,1)S(1)} %collective-permute-done.2), channel_id=1, source_target_pairs={{0,7},{1,0},{2,1},{3,2},{4,3},{5,4},{6,5},{7,6},{8,15},{9,8},{10,9... | collective-permute-start | bytes 393224 | tf_op jit(solution)/shard_map/ppermute | solution.py:17
  32.5 95.2 %collective-permute-start.6 = (bf16[2,128,256]{2,1,0:T(8,128)(2,1)S(1)}, bf16[2,128,256]{2,1,0:T(8,128)(2,1)S(1)}, u32[]{:S(2)}, u32[]{:S(2)}) collective-permute-start(bf16[2,128,256]{2,1,0:T(8,128)(2,1)S(1)} %collective-permute-done.5), channel_id=1, source_target_pairs={{0,1},{1,2},{2,3},{3,4},{4,5},{5,6},{6,7},{7,0},{8,9},{9,10},{10,1... | collective-permute-start | bytes 393224 | tf_op jit(solution)/shard_map/ppermute | solution.py:15
  120.5 4.8 %copy-start = (bf16[2048,2560]{0,1:T(8,128)(2,1)S(1)}, bf16[2048,2560]{0,1:T(8,128)(2,1)}, u32[]{:S(2)}) copy-start(bf16[2048,2560]{0,1:T(8,128)(2,1)} %all-gather.5.cloned.1.call-done) | copy-start | bytes 31457284
  129.4 128.0 %all-gather.11.cloned.1.call-start = ((), (), s32[]{:S(2)}) async-start(), calls=%async_computation.9 | async-start | bytes 3276800 | tf_op jit(solution)/shard_map/all_gather | solution.py:44
  161.8 159.8 %reduce-scatter.5.cloned.1.call-start = ((), (), s32[]{:S(2)}) async-start(), calls=%async_computation.7 | async-start | bytes 6553600 | tf_op jit(solution)/shard_map/reduce_scatter | solution.py:49
  253.4 132.4 %reduce-scatter.9.cloned.1.call-start = ((), (), s32[]{:S(2)}) async-start(), calls=%async_computation.10 | async-start | bytes 6553600 | tf_op jit(solution)/shard_map/reduce_scatter | solution.py:49
  294.4 126.3 %reduce-scatter.7.cloned.1.call-start = ((), (), s32[]{:S(2)}) async-start(), calls=%async_computation.8 | async-start | bytes 1179648 | tf_op jit(solution)/shard_map/reduce_scatter | solution.py:58
  328.6 64.2 %copy-start.2 = (f32[256]{0:T(256)S(1)}, f32[256]{0:T(256)}, u32[]{:S(2)}) copy-start(f32[256]{0:T(256)} %param.8) | copy-start | bytes 3076
  328.6 64.2 %copy-start.3 = (f32[128]{0:T(128)S(1)}, f32[128]{0:T(128)}, u32[]{:S(2)}) copy-start(f32[128]{0:T(128)} %param.7) | copy-start | bytes 1540
  328.6 125.2 %reduce-scatter.11.cloned.1.call-start = ((), (), s32[]{:S(2)}) async-start(), calls=%async_computation.11 | async-start | bytes 1179648 | tf_op jit(solution)/shard_map/reduce_scatter | solution.py:58
Sparse Core Ops, SparseCore 0:
  11.1 107.5 all-gather.4
  120.3 55.9 all-gather.8
  178.1 38.1 all-gather.6
  218.0 39.3 all-gather.10
  260.2 61.3 reduce-scatter.4
  324.4 61.3 reduce-scatter.8
  388.1 32.6 reduce-scatter.6
  423.0 30.7 reduce-scatter.10
